TPU v7x, 32 devices: a whole 2x2x4 slice. The times are simulated.
32 devices in a mesh: seq: 16 (over z, y, core), fsdp: 2 (over x).
Axes of the slice: x: 2, y: 2, z: 4, core: 2. Of those that a mesh axis runs over, the one named last changes fastest.
Arguments:
- tokens: bfloat16 [64, 8192], P('seq', 'fsdp'), may hold values from -6 to 6
- gate_weight: bfloat16 [8192, 16384], P('fsdp', 'seq'), may hold values from -0.0625 to 0.0625
- up_weight: bfloat16 [8192, 16384], P('fsdp', 'seq'), may hold values from -0.0625 to 0.0625
- down_weight: bfloat16 [8192, 16384], P('fsdp', 'seq'), may hold values from -0.046875 to 0.046875
Outputs:
- mixed_out: bfloat16 [64, 8192], P('seq', 'fsdp')
All inputs are finite; a program needn't handle non-finite values.
Results may differ from a plain program's by a relative error of at most 0.0049.
Values may be sent and summed in bfloat16 or wider, within the bound.
A program may use at most 64 MiB of HBM per device.

v0:
```python
import jax
import jax.numpy as jnp
from jax import lax
from jax.sharding import PartitionSpec as P


def project_down(hidden, weight):
    return lax.dot_general(
        hidden, weight, (((1,), (1,)), ((), ())), preferred_element_type=jnp.float32
    )


def on_device(tokens, gate_weight, up_weight, down_weight):
    units = gate_weight.shape[1]
    paired = jnp.concatenate([gate_weight, up_weight], axis=1)
    parts = jnp.dot(
        lax.all_gather(tokens, "seq", axis=0, tiled=True),
        paired,
        preferred_element_type=jnp.float32,
    )
    values = lax.psum(parts, "fsdp")
    hidden = (jax.nn.silu(values[:, :units]) * values[:, units:]).astype(jnp.bfloat16)
    return lax.psum_scatter(
        project_down(hidden, down_weight), "seq", scatter_dimension=0, tiled=True
    ).astype(jnp.bfloat16)


def solution(mesh):
    return jax.shard_map(
        on_device,
        mesh=mesh,
        in_specs=(P("seq", "fsdp"), P("fsdp", "seq"), P("fsdp", "seq"), P("fsdp", "seq")),
        out_specs=P("seq", "fsdp"),
        check_vma=False,
    )
```

profile of v0, /device:TPU:0, one launch (start us, length us, event | category | flops | bytes accessed | tf_op | source)
XLA Modules:
  0.0 152.2 jit_solution(14321686645150590111)
XLA Ops:
  6.5 0.0 all-reduce.4.cloned.1.call-start
  6.5 24.8 %all-gather = bf16[16,4,4096]{2,1,0:T(4,128)(2,1)S(1)} all-gather(bf16[1,4,4096]{2,1,0:T(4,128)(2,1)} %bitcast.6), channel_id=1, replica_groups=mesh['seq'=16,'fsdp'=2] {'seq'}, dimensions={0}, use_global_device_ids=true | all-gather | bytes 557056 | tf_op jit(solution)/shard_map/all_gather | solution.py:17
  31.3 0.1 reshape.1
  31.5 0.0 copy-start
  31.5 8.2 %fusion.4 = f32[64,2048]{1,0:T(8,128)} fusion(bf16[64,4096]{1,0:T(8,128)(2,1)S(1)} %reshape.1, bf16[4096,1024]{1,0:T(8,128)(2,1)} %param.6, bf16[4096,1024]{1,0:T(8,128)(2,1)} %param.5), kind=kOutput, calls=%fused_computation.4 | convolution fusion | flops 1107296256 | bytes 17825792 | tf_op jit(solution)/shard_map/dot_general | solution.py:16
  39.7 0.0 all-reduce.4.cloned.1.call-update
  39.8 0.0 copy-done
  39.8 0.6 dynamic-slice
  41.0 24.8 %all-reduce.4.cloned.1.call-done = f32[64,2048]{1,0:T(8,128)} async-done(((f32[64,2048]{1,0:T(8,128)}), f32[64,2048]{1,0:T(8,128)}) %all-reduce.4.cloned.1.call-update) | async-done | bytes 524304 | tf_op jit(solution)/shard_map/psum | solution.py:21
  65.8 6.2 %fusion.8 = f32[64,4096]{1,0:T(8,128)S(1)} fusion(bf16[4096,1024]{1,0:T(8,128)(2,1)} %param.7, f32[64,2048]{1,0:T(8,128)} %all-reduce.4.cloned.1.call-done), kind=kOutput, calls=%fused_computation.7 | convolution fusion | flops 537264128 | bytes 9961472 | tf_op jit(solution)/shard_map/dot_general | solution.py:8
  72.0 72.7 %all-reduce.5 = bf16[64,4096]{1,0:T(8,128)(2,1)S(1)} all-reduce(f32[64,4096]{1,0:T(8,128)S(1)} %fusion.8), channel_id=2, replica_groups=mesh['seq'=16,'fsdp'=2] {'seq'}, use_global_device_ids=true, to_apply=%region_1.2.clone | all-reduce | flops 262144 | bytes 1572864
  144.7 0.6 dynamic-slice_convert_fusion
Async XLA Ops:
  6.5 59.3 %all-reduce.4.cloned.1.call-start = ((), (), s32[]{:S(2)}) async-start(), calls=%async_computation | async-start | bytes 1048576 | tf_op jit(solution)/shard_map/psum | solution.py:21
  31.5 8.3 %copy-start = (u32[32]{0:T(128)S(1)}, u32[32]{0:T(128)}, u32[]{:S(2)}) copy-start(u32[32]{0:T(128)} %constant.6) | copy-start | bytes 388
Sparse Core Ops, SparseCore 0:
  39.9 25.8 all-reduce.3
where the time goes:
time: 152 us
  blocking collectives  97.5 us (64%)
  waiting for transfers between devices  24.8 us (16%)
  matrix products  14.5 us (10%)
  between operations  14.1 us (9%)
    unnamed x1, blocking collectives  72.7 us
    all_gather x1, blocking collectives, on_device(): lax.all_gather(tokens, 'seq', axis=0, tiled=True)  24.8 us
    psum x1, waiting for transfers between devices, on_device(): values = lax.psum(parts, 'fsdp')  24.8 us
    dot_general x1, matrix products, on_device(): jnp.dot(lax.all_gather(tokens, 'seq', axis=0, tiled=True), paired, prefer...  8.25 us
    dot_general x1, matrix products, project_down(): lax.dot_general(hidden, weight, (((1,), (1,)), ((), ())), preferred_eleme...  6.22 us
  transfers between devices with their start and end apart: 1, of which 1 were waited for; matrix products, arithmetic and copies ran while one was open for 0% of the time, Pallas kernels for 0%

commit v1 on v0

--- a/solution.py
+++ b/solution.py
@@ -18,7 +18,7 @@
         paired,
         preferred_element_type=jnp.float32,
     )
-    values = lax.psum(parts, "fsdp")
+    values = jnp.sum(lax.all_gather(parts, "fsdp"), axis=0)
     hidden = (jax.nn.silu(values[:, :units]) * values[:, units:]).astype(jnp.bfloat16)
     return lax.psum_scatter(
         project_down(hidden, down_weight), "seq", scatter_dimension=0, tiled=True

time: 152 us -> 146 us (0.961)
  waiting for transfers between devices: 24.8 us -> 17.5 us
    psum x1 -> x0, waiting for transfers between devices: 24.8 us -> none  [on_device(): values = lax.psum(parts, 'fsdp')]
    all_gather x0 -> x1, waiting for transfers between devices: none -> 17.4 us  [on_device(): values = jnp.sum(lax.all_gather(parts, 'fsdp'), axis=0)]
where the time goes in v1:
time: 146 us
  blocking collectives  97.5 us (67%)
  waiting for transfers between devices  17.5 us (12%)
  matrix products  14.3 us (10%)
  between operations  14.1 us (10%)
    unnamed x1, blocking collectives  72.7 us
    all_gather x1, blocking collectives, on_device(): lax.all_gather(tokens, 'seq', axis=0, tiled=True)  24.8 us
    all_gather x1, waiting for transfers between devices, on_device(): values = jnp.sum(lax.all_gather(parts, 'fsdp'), axis=0)  17.4 us
    dot_general x1, matrix products, on_device(): jnp.dot(lax.all_gather(tokens, 'seq', axis=0, tiled=True), paired, prefer...  8.26 us
    dot_general x1, matrix products, project_down(): lax.dot_general(hidden, weight, (((1,), (1,)), ((), ())), preferred_eleme...  6.04 us
  transfers between devices with their start and end apart: 1, of which 1 were waited for; matrix products, arithmetic and copies ran while one was open for 0% of the time, Pallas kernels for 0%

profile of v1, /device:TPU:0, one launch (start us, length us, event | category | flops | bytes accessed | tf_op | source)
XLA Modules:
  0.0 146.0 jit_solution(3553491815296364192)
XLA Ops:
  6.5 0.0 all-gather.4.cloned.1.call-start
  6.5 24.8 %all-gather.1 = bf16[16,4,4096]{2,1,0:T(4,128)(2,1)S(1)} all-gather(bf16[1,4,4096]{2,1,0:T(4,128)(2,1)} %bitcast.8), channel_id=1, replica_groups=mesh['seq'=16,'fsdp'=2] {'seq'}, dimensions={0}, use_global_device_ids=true | all-gather | bytes 557056 | tf_op jit(solution)/shard_map/all_gather | solution.py:17
  31.3 0.1 reshape.2
  31.5 0.0 copy-start
  31.5 8.3 %fusion.4 = f32[64,2048]{1,0:T(8,128)} fusion(bf16[64,4096]{1,0:T(8,128)(2,1)S(1)} %reshape.2, bf16[4096,1024]{1,0:T(8,128)(2,1)} %param.6, bf16[4096,1024]{1,0:T(8,128)(2,1)} %param.5), kind=kOutput, calls=%fused_computation.4 | convolution fusion | flops 1107296256 | bytes 17825792 | tf_op jit(solution)/shard_map/dot_general | solution.py:16
  39.7 0.0 all-gather.4.cloned.1.call-update
  39.8 0.0 copy-done
  39.8 0.6 dynamic-slice
  41.0 17.4 %all-gather.4.cloned.1.call-done = f32[128,2048]{1,0:T(8,128)} async-done(((f32[64,2048]{1,0:T(8,128)}), f32[128,2048]{1,0:T(8,128)}) %all-gather.4.cloned.1.call-update) | async-done | bytes 1048592 | tf_op jit(solution)/shard_map/all_gather | solution.py:21
  58.4 1.3 reduce_sum.9
  59.8 6.0 %fusion.8 = f32[64,4096]{1,0:T(8,128)S(1)} fusion(bf16[4096,1024]{1,0:T(8,128)(2,1)} %param.7, f32[64,2048]{1,0:T(8,128)S(1)} %reduce_sum.9), kind=kOutput, calls=%fused_computation.7 | convolution fusion | flops 537264128 | bytes 9961472 | tf_op jit(solution)/shard_map/dot_general | solution.py:8
  65.8 72.7 %all-reduce.2 = bf16[64,4096]{1,0:T(8,128)(2,1)S(1)} all-reduce(f32[64,4096]{1,0:T(8,128)S(1)} %fusion.8), channel_id=3, replica_groups=mesh['seq'=16,'fsdp'=2] {'seq'}, use_global_device_ids=true, to_apply=%region_1.2.clone | all-reduce | flops 262144 | bytes 1572864
  138.5 0.6 dynamic-slice_convert_fusion
Async XLA Ops:
  6.5 51.9 %all-gather.4.cloned.1.call-start = ((), (), s32[]{:S(2)}) async-start(), calls=%async_computation | async-start | bytes 1572864 | tf_op jit(solution)/shard_map/all_gather | solution.py:21
  31.5 8.3 %copy-start = (u32[32]{0:T(128)S(1)}, u32[32]{0:T(128)}, u32[]{:S(2)}) copy-start(u32[32]{0:T(128)} %constant.8) | copy-start | bytes 388
Sparse Core Ops, SparseCore 0:
  39.9 18.5 all-gather.3
